TPU v7x, 128 devices: a whole 4x4x4 slice. The times are simulated.
128 devices in a mesh: pb: 8 (over x, core), kv: 8 (over z_lo, y), ha: 2 (over z_hi).
Axes of the slice: x: 4, y: 4, z: 4 (z_hi: 2, z_lo: 2; z = z_hi * 2 + z_lo), core: 2. Of those that a mesh axis runs over, the one named last changes fastest.
Arguments:
- queries: bfloat16 [12288, 2048], P(('pb', 'kv', 'ha')), may hold values from -48 to 48
- keys: bfloat16 [12288, 2048], P(('pb', 'kv', 'ha')), may hold values from -6 to 6
- values: bfloat16 [12288, 2048], P(('pb', 'kv', 'ha')), may hold values from -6 to 6
- masked_at: int32 [3072], replicated, may hold values from 0 to 12287, as said below
- mask_query: bfloat16 [2048], replicated, may hold values from -6 to 6
- mask_key: bfloat16 [2048], replicated, may hold values from -6 to 6
- mask_value: bfloat16 [2048], replicated, may hold values from -6 to 6
Outputs:
- attended: bfloat16 [12288, 2048], P(('pb', 'kv', 'ha'))
Inputs may be any that keep to these rules, and one draw needn't show every extreme that they name: `masked_at`: 3072 distinct positions in rising order.
All inputs are finite; a program needn't handle non-finite values.
Results may differ from a plain program's by a relative error of at most 0.006.
Values may be sent and summed in bfloat16 or wider, within the bound.
No kernel may reach another device: no remote copies, remote signals or barrier semaphores. Data moves between devices by JAX's collectives and lax.ppermute only.
A program may use at most 128 MiB of HBM per device.

v0:
```python
import math

import jax
import jax.numpy as jnp
from jax import lax
from jax.sharding import PartitionSpec as P

DH = 128
HEADS = 16


rope_theta = 500000.0
very_negative = -1e30


def side_by_side(arrays, axis, dim, along):
    both = jnp.concatenate(arrays, axis=along)
    whole, at, gathered = (lax.all_gather(both, axis, axis=dim, tiled=True), 0, [])
    for a in arrays:
        gathered.append(lax.slice_in_dim(whole, at, at + a.shape[along], axis=along))
        at += a.shape[along]
    return tuple(gathered)


def rotated(vector, positions):
    halves = DH // 2
    exponent = jnp.arange(halves, dtype=jnp.float32) * (2.0 / DH)
    inverse = 1.0 / rope_theta**exponent
    angles = positions.astype(jnp.float32)[:, None] * inverse[None, :]
    cosine = jnp.cos(angles)[:, None, :]
    sine_part = jnp.sin(angles)[:, None, :]
    per_head = vector.astype(jnp.float32).reshape(HEADS, DH)
    first_half = per_head[None, :, :halves]
    second = per_head[None, :, halves:]
    result = jnp.concatenate(
        [first_half * cosine - second * sine_part, second * cosine + first_half * sine_part], axis=2
    )
    return result.reshape(positions.shape[0], HEADS * DH).astype(jnp.bfloat16)


def attend_piece(running, head_queries, piece_keys, piece_values, score_scale):
    head_total = head_queries.shape[0]

    def per_head(packed):
        head_index, query_part, old_max, old_total, old_sum = packed
        key_part = lax.dynamic_slice_in_dim(piece_keys, head_index * DH, DH, 1)
        value_part = lax.dynamic_slice_in_dim(piece_values, head_index * DH, DH, 1)
        scores = (
            jnp.einsum("qd,kd->qk", query_part, key_part, preferred_element_type=jnp.float32)
            * score_scale
        )
        new_max = jnp.maximum(old_max, jnp.max(scores, axis=1))
        factor = jnp.exp(old_max - new_max)
        weights = jnp.exp(scores - new_max[:, None])
        new_total = old_total * factor + jnp.sum(weights, axis=1)
        new_sum = old_sum * factor[:, None] + jnp.dot(
            weights.astype(jnp.bfloat16), value_part, preferred_element_type=jnp.float32
        )
        return (new_max, new_total, new_sum)

    return lax.map(
        per_head,
        (jnp.arange(head_total, dtype=jnp.int32), head_queries, running[0], running[1], running[2]),
    )


def finish(received):
    part_max, part_total, part_sum = received
    joint_max = jnp.max(part_max, axis=0)
    factor = jnp.exp(part_max - joint_max[None])
    total_sum = jnp.sum(part_total * factor, axis=0)
    summed = jnp.sum(part_sum * factor[..., None], axis=0)
    return summed / total_sum[..., None]


def starting(head_total, query_total):
    return (
        jnp.full((head_total, query_total), very_negative, jnp.float32),
        jnp.zeros((head_total, query_total), jnp.float32),
        jnp.zeros((head_total, query_total, DH), jnp.float32),
    )


def body(queries, keys, values, masked_at, mask_query, mask_key, mask_value):
    local_rows = queries.shape[0]
    full_width = queries.shape[1]
    first_row = lax.axis_index(("pb", "kv", "ha")) * local_rows
    positions = first_row + jnp.arange(local_rows, dtype=jnp.int32)
    masked_flags = jnp.any(positions[:, None] == masked_at[None, :], axis=1)
    query_used = jnp.where(masked_flags[:, None], rotated(mask_query, positions), queries)
    key_used = jnp.where(masked_flags[:, None], rotated(mask_key, positions), keys)
    value_used = jnp.where(masked_flags[:, None], mask_value[None, :], values)
    group_width = full_width // lax.axis_size("ha")
    head_total = group_width // DH
    score_scale = 1.0 / math.sqrt(DH)
    query_group, key_group, value_group = (
        lax.all_to_all(query_used, "ha", split_axis=1, concat_axis=0, tiled=True),
        lax.all_to_all(key_used, "ha", split_axis=1, concat_axis=0, tiled=True),
        lax.all_to_all(value_used, "ha", split_axis=1, concat_axis=0, tiled=True),
    )
    own_queries = lax.all_gather(query_group, "kv", axis=0, tiled=True)
    query_total = own_queries.shape[0]
    head_queries = own_queries.reshape(query_total, head_total, DH).transpose(1, 0, 2)
    portion = side_by_side((key_group, value_group), "pb", 0, 1)
    running = attend_piece(
        starting(head_total, query_total), head_queries, portion[0], portion[1], score_scale
    )
    owned_rows = query_total // lax.axis_size("kv")
    stacked = (running[0][None], running[1][None], running[2][None])
    normalized = finish(
        (
            lax.all_to_all(stacked[0], "kv", split_axis=2, concat_axis=0, tiled=True),
            lax.all_to_all(stacked[1], "kv", split_axis=2, concat_axis=0, tiled=True),
            lax.all_to_all(stacked[2], "kv", split_axis=2, concat_axis=0, tiled=True),
        )
    )
    out_rows = normalized.transpose(1, 0, 2).reshape(owned_rows, group_width).astype(jnp.bfloat16)
    return lax.all_to_all(out_rows, "ha", split_axis=0, concat_axis=1, tiled=True)


def solution(mesh):
    in_specs = (
        P(("pb", "kv", "ha"), None),
        P(("pb", "kv", "ha"), None),
        P(("pb", "kv", "ha"), None),
        P(),
        P(),
        P(),
        P(),
    )
    out_specs = P(("pb", "kv", "ha"), None)
    return jax.shard_map(body, mesh=mesh, in_specs=in_specs, out_specs=out_specs, check_vma=False)
```

profile of v0, /device:TPU:24, one launch (start us, length us, event | category | flops | bytes accessed | tf_op | source)
XLA Modules:
  0.0 589.7 jit_solution(16703127739279018998)
XLA Ops:
  11.7 13.1 %all_to_all.127 = bf16[96,2,1024]{2,0,1:T(8,128)(2,1)} all-to-all(bf16[96,2,1024]{2,0,1:T(8,128)(2,1)S(1)} %bitcast.98), channel_id=1, replica_groups=mesh['pb'=8,'kv'=8,'ha'=2] {'ha'}, dimensions={1} | all-to-all | bytes 786432 | tf_op jit(solution)/shard_map/all_to_all | solution.py:97
  25.6 3.5 all-to-all-start.2
  29.2 11.5 %all-to-all-done.2 = bf16[96,2,1024]{2,0,1:T(8,128)(2,1)S(1)} async-done(((bf16[96,2,1024]{2,0,1:T(8,128)(2,1)}), bf16[96,2,1024]{2,0,1:T(8,128)(2,1)S(1)}, u32[]{:S(2)}, u32[]{:S(2)}) %all-to-all-start.2) | async-done | bytes 393248 | tf_op jit(solution)/shard_map/all_to_all | solution.py:99
  40.7 29.5 %all_to_all.128 = bf16[96,2,1024]{2,0,1:T(8,128)(2,1)S(1)} all-to-all(bf16[96,2,1024]{2,0,1:T(8,128)(2,1)S(1)} %bitcast.97), channel_id=1, replica_groups=mesh['pb'=8,'kv'=8,'ha'=2] {'ha'}, dimensions={1} | all-to-all | bytes 786432 | tf_op jit(solution)/shard_map/all_to_all | solution.py:98
  71.3 4.7 copy.34
  76.0 35.1 %all-gather.5.cloned.1.call-done = bf16[1536,2048]{1,0:T(8,128)(2,1)} async-done(((bf16[192,2048]{1,0:T(8,128)(2,1)}), bf16[1536,2048]{1,0:T(8,128)(2,1)}) %all-gather.5.cloned.1.call-update) | async-done | bytes 6291472 | tf_op jit(solution)/shard_map/all_gather | solution.py:18
  111.0 6.1 %fusion.21 = (bf16[1536,1024]{1,0:T(8,128)(2,1)}, bf16[1536,1024]{1,0:T(8,128)(2,1)}) fusion(bf16[1536,2048]{1,0:T(8,128)(2,1)} %all-gather.5.cloned.1.call-done), kind=kLoop, calls=%fused_computation.47 | loop fusion | bytes 12582912 | tf_op jit(solution)/shard_map/slice | solution.py:20
  117.2 319.7 %while.14 = (s32[]{:T(128)}, f32[8,1536]{1,0:T(8,128)S(1)}, f32[8,1536]{1,0:T(8,128)S(1)}, f32[8,1536,128]{2,0,1:T(8,128)}, bf16[8,1536,128]{1,2,0:T(8,128)(2,1)...) while((s32[]{:T(128)}, f32[8,1536]{1,0:T(8,128)S(1)}, ...), condition=%wide.region_4.5_spmd, body=%wide.region_1.4_spmd.sunk | while | flops 1222318080 | bytes 31955152 | solution.py:61
  118.6 6.1 %fusion.31 = (f32[1536]{0:T(1024)S(1)}, f32[1536,1536]{0,1:T(8,128)}) fusion(bf16[8,1536,128]{1,2,0:T(8,128)(2,1)} %get-tuple-element.212, s32[]{:T(128)S(6)} %copy.73, bf16[1536,1024]{1,0:T(8,128)(2,1)} %get-tuple-element.214, s32[]{:T(128)S(6)} %select_n.22), kind=kOutput, calls=%fused_computation.46.clone.1 | convolution fusion | flops 608696832 | bytes 10229768 | tf_op jit(solution)/shard_map/while/body/eval_jaxpr/qd,kd->qk/dot_general | solution.py:49
  124.9 5.0 fusion.32
  130.1 5.5 fusion.33
  135.6 21.6 %dynamic_update_slice.16 = f32[8,1536,128]{2,0,1:T(8,128)} dynamic-update-slice(f32[8,1536,128]{2,0,1:T(8,128)} %get-tuple-element.199, f32[1,1536,128]{2,0,1:T(1,128)S(1)} %bitcast.90, s32[]{:T(128)S(6)} %copy.73, s32[]{:T(128)} %constant.30.clone.1..sunk, s32[]{:T(128)} %constant.30.clone.1..sunk) | dynamic-update-slice | bytes 1572868 | tf_op jit(solution)/shard_map/while/body/jit(dynamic_update_index_in_dim)/dynamic_update_slice | solution.py:61
  158.5 6.1 %fusion.31 = (f32[1536]{0:T(1024)S(1)}, f32[1536,1536]{0,1:T(8,128)}) fusion(bf16[8,1536,128]{1,2,0:T(8,128)(2,1)} %get-tuple-element.212, s32[]{:T(128)S(6)} %copy.73, bf16[1536,1024]{1,0:T(8,128)(2,1)} %get-tuple-element.214, s32[]{:T(128)S(6)} %select_n.22), kind=kOutput, calls=%fused_computation.46.clone.1 | convolution fusion | flops 608696832 | bytes 10229768 | tf_op jit(solution)/shard_map/while/body/eval_jaxpr/qd,kd->qk/dot_general | solution.py:49
  164.8 5.0 fusion.32
  170.0 5.5 fusion.33
  175.5 21.6 %dynamic_update_slice.16 = f32[8,1536,128]{2,0,1:T(8,128)} dynamic-update-slice(f32[8,1536,128]{2,0,1:T(8,128)} %get-tuple-element.199, f32[1,1536,128]{2,0,1:T(1,128)S(1)} %bitcast.90, s32[]{:T(128)S(6)} %copy.73, s32[]{:T(128)} %constant.30.clone.1..sunk, s32[]{:T(128)} %constant.30.clone.1..sunk) | dynamic-update-slice | bytes 1572868 | tf_op jit(solution)/shard_map/while/body/jit(dynamic_update_index_in_dim)/dynamic_update_slice | solution.py:61
  198.5 6.1 %fusion.31 = (f32[1536]{0:T(1024)S(1)}, f32[1536,1536]{0,1:T(8,128)}) fusion(bf16[8,1536,128]{1,2,0:T(8,128)(2,1)} %get-tuple-element.212, s32[]{:T(128)S(6)} %copy.73, bf16[1536,1024]{1,0:T(8,128)(2,1)} %get-tuple-element.214, s32[]{:T(128)S(6)} %select_n.22), kind=kOutput, calls=%fused_computation.46.clone.1 | convolution fusion | flops 608696832 | bytes 10229768 | tf_op jit(solution)/shard_map/while/body/eval_jaxpr/qd,kd->qk/dot_general | solution.py:49
  204.8 5.0 fusion.32
  210.0 5.5 fusion.33
  215.5 21.6 %dynamic_update_slice.16 = f32[8,1536,128]{2,0,1:T(8,128)} dynamic-update-slice(f32[8,1536,128]{2,0,1:T(8,128)} %get-tuple-element.199, f32[1,1536,128]{2,0,1:T(1,128)S(1)} %bitcast.90, s32[]{:T(128)S(6)} %copy.73, s32[]{:T(128)} %constant.30.clone.1..sunk, s32[]{:T(128)} %constant.30.clone.1..sunk) | dynamic-update-slice | bytes 1572868 | tf_op jit(solution)/shard_map/while/body/jit(dynamic_update_index_in_dim)/dynamic_update_slice | solution.py:61
  238.5 6.1 %fusion.31 = (f32[1536]{0:T(1024)S(1)}, f32[1536,1536]{0,1:T(8,128)}) fusion(bf16[8,1536,128]{1,2,0:T(8,128)(2,1)} %get-tuple-element.212, s32[]{:T(128)S(6)} %copy.73, bf16[1536,1024]{1,0:T(8,128)(2,1)} %get-tuple-element.214, s32[]{:T(128)S(6)} %select_n.22), kind=kOutput, calls=%fused_computation.46.clone.1 | convolution fusion | flops 608696832 | bytes 10229768 | tf_op jit(solution)/shard_map/while/body/eval_jaxpr/qd,kd->qk/dot_general | solution.py:49
  244.8 5.0 fusion.32
  249.9 5.5 fusion.33
  255.5 21.6 %dynamic_update_slice.16 = f32[8,1536,128]{2,0,1:T(8,128)} dynamic-update-slice(f32[8,1536,128]{2,0,1:T(8,128)} %get-tuple-element.199, f32[1,1536,128]{2,0,1:T(1,128)S(1)} %bitcast.90, s32[]{:T(128)S(6)} %copy.73, s32[]{:T(128)} %constant.30.clone.1..sunk, s32[]{:T(128)} %constant.30.clone.1..sunk) | dynamic-update-slice | bytes 1572868 | tf_op jit(solution)/shard_map/while/body/jit(dynamic_update_index_in_dim)/dynamic_update_slice | solution.py:61
  278.4 6.1 %fusion.31 = (f32[1536]{0:T(1024)S(1)}, f32[1536,1536]{0,1:T(8,128)}) fusion(bf16[8,1536,128]{1,2,0:T(8,128)(2,1)} %get-tuple-element.212, s32[]{:T(128)S(6)} %copy.73, bf16[1536,1024]{1,0:T(8,128)(2,1)} %get-tuple-element.214, s32[]{:T(128)S(6)} %select_n.22), kind=kOutput, calls=%fused_computation.46.clone.1 | convolution fusion | flops 608696832 | bytes 10229768 | tf_op jit(solution)/shard_map/while/body/eval_jaxpr/qd,kd->qk/dot_general | solution.py:49
  284.7 5.0 fusion.32
  289.9 5.5 fusion.33
  295.4 21.6 %dynamic_update_slice.16 = f32[8,1536,128]{2,0,1:T(8,128)} dynamic-update-slice(f32[8,1536,128]{2,0,1:T(8,128)} %get-tuple-element.199, f32[1,1536,128]{2,0,1:T(1,128)S(1)} %bitcast.90, s32[]{:T(128)S(6)} %copy.73, s32[]{:T(128)} %constant.30.clone.1..sunk, s32[]{:T(128)} %constant.30.clone.1..sunk) | dynamic-update-slice | bytes 1572868 | tf_op jit(solution)/shard_map/while/body/jit(dynamic_update_index_in_dim)/dynamic_update_slice | solution.py:61
  318.4 6.1 %fusion.31 = (f32[1536]{0:T(1024)S(1)}, f32[1536,1536]{0,1:T(8,128)}) fusion(bf16[8,1536,128]{1,2,0:T(8,128)(2,1)} %get-tuple-element.212, s32[]{:T(128)S(6)} %copy.73, bf16[1536,1024]{1,0:T(8,128)(2,1)} %get-tuple-element.214, s32[]{:T(128)S(6)} %select_n.22), kind=kOutput, calls=%fused_computation.46.clone.1 | convolution fusion | flops 608696832 | bytes 10229768 | tf_op jit(solution)/shard_map/while/body/eval_jaxpr/qd,kd->qk/dot_general | solution.py:49
  324.7 5.0 fusion.32
  329.9 5.6 fusion.33
  335.4 21.6 %dynamic_update_slice.16 = f32[8,1536,128]{2,0,1:T(8,128)} dynamic-update-slice(f32[8,1536,128]{2,0,1:T(8,128)} %get-tuple-element.199, f32[1,1536,128]{2,0,1:T(1,128)S(1)} %bitcast.90, s32[]{:T(128)S(6)} %copy.73, s32[]{:T(128)} %constant.30.clone.1..sunk, s32[]{:T(128)} %constant.30.clone.1..sunk) | dynamic-update-slice | bytes 1572868 | tf_op jit(solution)/shard_map/while/body/jit(dynamic_update_index_in_dim)/dynamic_update_slice | solution.py:61
  358.4 6.1 %fusion.31 = (f32[1536]{0:T(1024)S(1)}, f32[1536,1536]{0,1:T(8,128)}) fusion(bf16[8,1536,128]{1,2,0:T(8,128)(2,1)} %get-tuple-element.212, s32[]{:T(128)S(6)} %copy.73, bf16[1536,1024]{1,0:T(8,128)(2,1)} %get-tuple-element.214, s32[]{:T(128)S(6)} %select_n.22), kind=kOutput, calls=%fused_computation.46.clone.1 | convolution fusion | flops 608696832 | bytes 10229768 | tf_op jit(solution)/shard_map/while/body/eval_jaxpr/qd,kd->qk/dot_general | solution.py:49
  364.7 5.0 fusion.32
  369.9 5.5 fusion.33
  375.4 21.6 %dynamic_update_slice.16 = f32[8,1536,128]{2,0,1:T(8,128)} dynamic-update-slice(f32[8,1536,128]{2,0,1:T(8,128)} %get-tuple-element.199, f32[1,1536,128]{2,0,1:T(1,128)S(1)} %bitcast.90, s32[]{:T(128)S(6)} %copy.73, s32[]{:T(128)} %constant.30.clone.1..sunk, s32[]{:T(128)} %constant.30.clone.1..sunk) | dynamic-update-slice | bytes 1572868 | tf_op jit(solution)/shard_map/while/body/jit(dynamic_update_index_in_dim)/dynamic_update_slice | solution.py:61
  398.3 6.1 %fusion.31 = (f32[1536]{0:T(1024)S(1)}, f32[1536,1536]{0,1:T(8,128)}) fusion(bf16[8,1536,128]{1,2,0:T(8,128)(2,1)} %get-tuple-element.212, s32[]{:T(128)S(6)} %copy.73, bf16[1536,1024]{1,0:T(8,128)(2,1)} %get-tuple-element.214, s32[]{:T(128)S(6)} %select_n.22), kind=kOutput, calls=%fused_computation.46.clone.1 | convolution fusion | flops 608696832 | bytes 10229768 | tf_op jit(solution)/shard_map/while/body/eval_jaxpr/qd,kd->qk/dot_general | solution.py:49
  404.6 5.0 fusion.32
  409.8 5.5 fusion.33
  415.3 21.6 %dynamic_update_slice.16 = f32[8,1536,128]{2,0,1:T(8,128)} dynamic-update-slice(f32[8,1536,128]{2,0,1:T(8,128)} %get-tuple-element.199, f32[1,1536,128]{2,0,1:T(1,128)S(1)} %bitcast.90, s32[]{:T(128)S(6)} %copy.73, s32[]{:T(128)} %constant.30.clone.1..sunk, s32[]{:T(128)} %constant.30.clone.1..sunk) | dynamic-update-slice | bytes 1572868 | tf_op jit(solution)/shard_map/while/body/jit(dynamic_update_index_in_dim)/dynamic_update_slice | solution.py:61
  437.7 7.1 %reduce.1 = f32[1536,8]{1,0:T(8,128)S(1)} reduce(f32[1536,1,8]{2,1,0:T(1,128)S(1)} %bitcast.92, f32[]{:T(128)} %broadcast.133), dimensions={1}, to_apply=%bitcast.76.reduce_sub_computation | reduce | bytes 98308
  445.8 5.8 all-to-all-start.5
  451.9 7.1 %reduce.3 = f32[1536,8]{1,0:T(8,128)S(1)} reduce(f32[1536,1,8]{2,1,0:T(1,128)S(1)} %bitcast.93, f32[]{:T(128)} %broadcast.133), dimensions={1}, to_apply=%bitcast.74.reduce_sub_computation | reduce | bytes 98308
  459.4 9.8 %all_to_all.129 = f32[8,1,1536]{2,1,0:T(1,128)S(1)} all-to-all(f32[8,1,1536]{2,1,0:T(1,128)S(1)} %reshape.156), channel_id=1, replica_groups=mesh['pb'=8,'kv'=8,'ha'=2] {'kv'}, dimensions={0} | all-to-all | bytes 98304 | tf_op jit(solution)/shard_map/all_to_all | solution.py:112
  469.2 6.6 %all-to-all-start.3 = ((f32[1,8,1536,128]{3,1,0,2:T(8,128)}), f32[1,8,1536,128]{3,1,0,2:T(8,128)}, u32[]{:S(2)}, u32[]{:S(2)}) async-start(f32[1,8,1536,128]{3,1,0,2:T(8,128)} %bitcast.91), calls=%async_computation.3 | async-start | bytes 12582912 | tf_op jit(solution)/shard_map/all_to_all | solution.py:114
  480.4 84.7 %all-to-all-done.3 = f32[1,8,1536,128]{3,1,0,2:T(8,128)} async-done(((f32[1,8,1536,128]{3,1,0,2:T(8,128)}), f32[1,8,1536,128]{3,1,0,2:T(8,128)}, u32[]{:S(2)}, u32[]{:S(2)}) %all-to-all-start.3) | async-done | bytes 6291488 | tf_op jit(solution)/shard_map/all_to_all | solution.py:114
  565.0 5.0 fusion.14
  570.8 11.4 %all_to_all.130 = bf16[2,96,1024]{2,1,0:T(8,128)(2,1)S(1)} all-to-all(bf16[2,96,1024]{2,1,0:T(8,128)(2,1)S(1)} %convert_element_type.32), channel_id=1, replica_groups=mesh['pb'=8,'kv'=8,'ha'=2] {'ha'}, dimensions={0} | all-to-all | bytes 786432 | tf_op jit(solution)/shard_map/all_to_all | solution.py:118
  (90 shorter events, 23.5 us)
Async XLA Ops:
  6.5 64.7 %all-gather.3.cloned.1.call-start = ((), (), s32[]{:S(2)}) async-start(), calls=%async_computation.7 | async-start | bytes 3538944 | tf_op jit(solution)/shard_map/all_gather | solution.py:101
  25.6 15.1 %all-to-all-start.2 = ((bf16[96,2,1024]{2,0,1:T(8,128)(2,1)}), bf16[96,2,1024]{2,0,1:T(8,128)(2,1)S(1)}, u32[]{:S(2)}, u32[]{:S(2)}) async-start(bf16[96,2,1024]{2,0,1:T(8,128)(2,1)} %bitcast.81), calls=%async_computation.2 | async-start | bytes 786432 | tf_op jit(solution)/shard_map/all_to_all | solution.py:99
  29.1 81.9 %all-gather.5.cloned.1.call-start = ((), (), s32[]{:S(2)}) async-start(), calls=%async_computation.8 | async-start | bytes 7077888 | tf_op jit(solution)/shard_map/all_gather | solution.py:18
  445.8 13.6 %all-to-all-start.5 = ((f32[8,1,1536]{2,1,0:T(1,128)}), f32[8,1,1536]{2,1,0:T(1,128)S(1)}, u32[]{:S(2)}, u32[]{:S(2)}) async-start(f32[8,1,1536]{2,1,0:T(1,128)} %reshape.158), calls=%async_computation.5 | async-start | bytes 98304 | tf_op jit(solution)/shard_map/all_to_all | solution.py:113
  469.2 95.9 %all-to-all-start.3 = ((f32[1,8,1536,128]{3,1,0,2:T(8,128)}), f32[1,8,1536,128]{3,1,0,2:T(8,128)}, u32[]{:S(2)}, u32[]{:S(2)}) async-start(f32[1,8,1536,128]{3,1,0,2:T(8,128)} %bitcast.91), calls=%async_computation.3 | async-start | bytes 12582912 | tf_op jit(solution)/shard_map/all_to_all | solution.py:114
Sparse Core Ops, SparseCore 0:
  25.0 41.8 all-gather.2
  71.3 39.6 all-gather.4
where the time goes:
time: 595 us; the launch traced here: 590 us
  local copies, waits for them, and re-layouts  199 us (33%)
  waiting for transfers between devices  131 us (22%)
  matrix products  93.2 us (16%)
  other arithmetic  67 us (11%)
  blocking collectives  63.8 us (11%)
  starting transfers between devices  15.9 us (3%)
  between operations  13.6 us (2%)
    dynamic_update_slice x24, local copies, waits for them, and re-layouts, attend_piece(): lax.map(per_head, (jnp.arange(head_total, dtype=jnp.int32), head_queries,...  175 us
    all_to_all x1, waiting for transfers between devices, body(): lax.all_to_all(stacked[2], 'kv', split_axis=2, concat_axis=0, tiled=True)  84.7 us
    dot_general x8, matrix products, per_head(): jnp.einsum('qd,kd->qk', query_part, key_part, preferred_element_type=jnp....  49.1 us
    dot_general x8, matrix products, per_head(): jnp.dot(weights.astype(jnp.bfloat16), value_part, preferred_element_type=...  44.2 us
    reduce_sum x8, other arithmetic, per_head(): new_total = old_total * factor + jnp.sum(weights, axis=1)  39.9 us
    all_gather x1, waiting for transfers between devices, side_by_side(): lax.all_gather(both, axis, axis=dim, tiled=True)  35.1 us
    all_to_all x1, blocking collectives, body(): lax.all_to_all(key_used, 'ha', split_axis=1, concat_axis=0, tiled=True)  29.5 us
    unnamed x2, other arithmetic  14.2 us
  transfers between devices with their start and end apart: 5, of which 3 were waited for; matrix products, arithmetic and copies ran while one was open for 3% of the time, Pallas kernels for 0%

commit v1 on v0

v1 whole, which is shorter than its diff:
```python
import functools
import math

import jax
import jax.numpy as jnp
from jax import lax
from jax.experimental import pallas as pl
from jax.experimental.pallas import tpu as pltpu
from jax.sharding import PartitionSpec as P

DH = 128
HEADS = 16
ROPE_THETA = 500000.0
VERY_NEGATIVE = -1e30
SAFE_SCORE = 100.0
SCORE_SCALE = math.log2(math.e) / math.sqrt(DH)
CONTRACT_LAST = (((1,), (1,)), ((), ()))
PLANE = ("kv", "ha")


def rotated(vector, positions):
    halves = DH // 2
    exponent = jnp.arange(halves, dtype=jnp.float32) * (2.0 / DH)
    inverse = 1.0 / ROPE_THETA**exponent
    angles = positions.astype(jnp.float32)[:, None] * inverse[None, :]
    cosine = jnp.cos(angles)[:, None, :]
    sine_part = jnp.sin(angles)[:, None, :]
    per_head = vector.astype(jnp.float32).reshape(HEADS, DH)
    first_half = per_head[None, :, :halves]
    second = per_head[None, :, halves:]
    result = jnp.concatenate(
        [first_half * cosine - second * sine_part, second * cosine + first_half * sine_part], axis=2
    )
    return result.reshape(positions.shape[0], HEADS * DH).astype(jnp.bfloat16)


def along_x(x, step):
    return lax.ppermute(x, "pb", [(i, (i + 2 * step) % 8) for i in range(8)])


def other_core(x):
    return lax.ppermute(x, "pb", [(i, i ^ 1) for i in range(8)])


def row_norm_max(rows):
    wide = rows.astype(jnp.float32)
    return jnp.max(jnp.sum(wide * wide, axis=1, keepdims=True))


def split_kernel(q_ref, out_ref, norm_ref):
    scaled = q_ref[...].astype(jnp.float32) * SCORE_SCALE
    high = scaled.astype(jnp.bfloat16)
    low = (scaled - high.astype(jnp.float32)).astype(jnp.bfloat16)
    out_ref[:, :DH] = high
    out_ref[:, DH:] = low
    norm_ref[0, 0] = row_norm_max(scaled)


def split_queries(q):
    rows = q.shape[0]
    return pl.pallas_call(
        split_kernel,
        in_specs=[pl.BlockSpec(memory_space=pltpu.VMEM)],
        out_specs=[pl.BlockSpec(memory_space=pltpu.VMEM), pl.BlockSpec(memory_space=pltpu.SMEM)],
        out_shape=[
            jax.ShapeDtypeStruct((rows, 2 * DH), jnp.bfloat16),
            jax.ShapeDtypeStruct((1, 1), jnp.float32),
        ],
        name="split_queries",
    )(q)


def attend_kernel(*refs, pieces, first, key_tile, query_tile):
    norm_ref, q_ref = refs[:2]
    key_refs = refs[2 : 2 + pieces]
    value_refs = refs[2 + pieces : 2 + 2 * pieces]
    rest = refs[2 + 2 * pieces :]
    if not first:
        flag_in, sum_in, total_in, max_in = rest[:4]
        rest = rest[4:]
    flag_out, sum_out, total_out, max_out, turned_ref, weight_ref, safe_ref = rest
    piece_rows = key_refs[0].shape[0]
    rows = q_ref.shape[0]

    @pl.when(pl.program_id(0) == 0)
    def _():
        largest = 0.0
        for piece in range(pieces):
            turned_ref[:, pl.ds(piece * piece_rows, piece_rows)] = value_refs[piece][...].T
            largest = jnp.maximum(largest, row_norm_max(key_refs[piece][...]))
        safe = (largest * norm_ref[0, 0] * 1.02 < SAFE_SCORE * SAFE_SCORE).astype(jnp.int32)
        if not first:
            safe = safe * flag_in[0, 0]
        safe_ref[0] = safe
        flag_out[0, 0] = safe

    def doubled(piece, start, size):
        tile = key_refs[piece][pl.ds(start, size), :]
        return jnp.concatenate([tile, tile], axis=1)

    @pl.when(safe_ref[0] == 1)
    def _():
        max_out[...] = jnp.zeros(max_out.shape, jnp.float32)
        for block in range(rows // query_tile):
            columns = pl.ds(block * query_tile, query_tile)
            queries = q_ref[columns, :]
            total = None if first else total_in[:, columns]
            for piece in range(pieces):
                for tile in range(piece_rows // key_tile):
                    scores = lax.dot_general(
                        doubled(piece, tile * key_tile, key_tile),
                        queries,
                        CONTRACT_LAST,
                        preferred_element_type=jnp.float32,
                    )
                    weights = jnp.exp2(scores)
                    part = weights.reshape(key_tile // 8, 8, query_tile).sum(axis=0)
                    total = part if total is None else total + part
                    weight_ref[block % 2, pl.ds(piece * piece_rows + tile * key_tile, key_tile), :] = (
                        weights.astype(jnp.bfloat16)
                    )
            summed = jnp.dot(turned_ref[...], weight_ref[block % 2], preferred_element_type=jnp.float32)
            if not first:
                summed = summed + sum_in[:, columns]
            sum_out[:, columns] = summed
            total_out[:, columns] = total

    @pl.when(safe_ref[0] == 0)
    def _():
        if first:
            sum_out[...] = jnp.zeros(sum_out.shape, jnp.float32)
            total_out[...] = jnp.zeros(total_out.shape, jnp.float32)
            max_out[...] = jnp.full(max_out.shape, VERY_NEGATIVE, jnp.float32)
        else:
            sum_out[...] = sum_in[...]
            total_out[...] = total_in[...]
            max_out[...] = max_in[...]
        small = 128
        for piece in range(pieces):

            def one_tile(index, carry):
                start = pl.multiple_of((index // (rows // small)) * small, small)
                columns = pl.ds(pl.multiple_of((index % (rows // small)) * small, small), small)
                scores = lax.dot_general(
                    doubled(piece, start, small),
                    q_ref[columns, :],
                    CONTRACT_LAST,
                    preferred_element_type=jnp.float32,
                )
                old_max = max_out[:1, columns]
                new_max = jnp.maximum(old_max, jnp.max(scores, axis=0, keepdims=True))
                factor = jnp.exp2(old_max - new_max)
                weights = jnp.exp2(scores - new_max)
                total_out[:, columns] = total_out[:, columns] * factor + weights.reshape(
                    small // 8, 8, small
                ).sum(axis=0)
                sum_out[:, columns] = sum_out[:, columns] * factor + lax.dot_general(
                    value_refs[piece][pl.ds(start, small), :],
                    weights.astype(jnp.bfloat16),
                    (((0,), (0,)), ((), ())),
                    preferred_element_type=jnp.float32,
                )
                max_out[:, columns] = jnp.broadcast_to(new_max, (8, small))
                return carry

            lax.fori_loop(0, (piece_rows // small) * (rows // small), one_tile, 0)


def attend(norm, queries, keys, values, state, name, block=768, key_tile=512, query_tile=384):
    rows = queries.shape[0]
    pieces = len(keys)
    piece_rows = keys[0].shape[0]
    first = state is None
    scalar = pl.BlockSpec(memory_space=pltpu.SMEM)
    whole = pl.BlockSpec((piece_rows, DH), lambda i: (0, 0))
    state_specs = [
        scalar,
        pl.BlockSpec((DH, block), lambda i: (0, i)),
        pl.BlockSpec((8, block), lambda i: (0, i)),
        pl.BlockSpec((8, block), lambda i: (0, i)),
    ]
    in_specs = [scalar, pl.BlockSpec((block, 2 * DH), lambda i: (i, 0))] + [whole] * (2 * pieces)
    operands = [norm, queries, *keys, *values]
    aliases = {}
    if not first:
        aliases = {len(operands) + i: i for i in range(1, 4)}
        in_specs += state_specs
        operands += list(state)
    return pl.pallas_call(
        functools.partial(
            attend_kernel, pieces=pieces, first=first, key_tile=key_tile, query_tile=query_tile
        ),
        grid=(rows // block,),
        in_specs=in_specs,
        out_specs=state_specs,
        out_shape=[
            jax.ShapeDtypeStruct((1, 1), jnp.int32),
            jax.ShapeDtypeStruct((DH, rows), jnp.float32),
            jax.ShapeDtypeStruct((8, rows), jnp.float32),
            jax.ShapeDtypeStruct((8, rows), jnp.float32),
        ],
        scratch_shapes=[
            pltpu.VMEM((DH, pieces * piece_rows), jnp.bfloat16),
            pltpu.VMEM((2, pieces * piece_rows, query_tile), jnp.bfloat16),
            pltpu.SMEM((1,), jnp.int32),
        ],
        input_output_aliases=aliases,
        compiler_params=pltpu.CompilerParams(vmem_limit_bytes=48 * 2**20),
        name=name,
    )(*operands)


def finish_kernel(sum_a, total_a, max_a, sum_b, total_b, max_b, out_ref):
    joint = jnp.maximum(max_a[...], max_b[...])
    factor_a = jnp.exp2(max_a[...] - joint)
    factor_b = jnp.exp2(max_b[...] - joint)
    total = jnp.sum(total_a[...] * factor_a + total_b[...] * factor_b, axis=0, keepdims=True)
    summed = sum_a[...] * factor_a[:1] + sum_b[...] * factor_b[:1]
    out_ref[...] = (summed / total).T.astype(jnp.bfloat16)


def finish(own, received):
    rows = own[0].shape[1]
    return pl.pallas_call(
        finish_kernel,
        in_specs=[pl.BlockSpec(memory_space=pltpu.VMEM)] * 6,
        out_specs=pl.BlockSpec(memory_space=pltpu.VMEM),
        out_shape=jax.ShapeDtypeStruct((rows, DH), jnp.bfloat16),
        compiler_params=pltpu.CompilerParams(vmem_limit_bytes=48 * 2**20),
        name="finish",
    )(*own, *received)


def to_heads(x):
    return lax.all_to_all(x, PLANE, split_axis=1, concat_axis=0, tiled=True)


def body(queries, keys, values, masked_at, mask_query, mask_key, mask_value):
    local_rows = queries.shape[0]
    first_row = lax.axis_index(("pb", "kv", "ha")) * local_rows
    positions = first_row + jnp.arange(local_rows, dtype=jnp.int32)
    masked_flags = jnp.any(positions[:, None] == masked_at[None, :], axis=1)
    key_used = jnp.where(masked_flags[:, None], rotated(mask_key, positions), keys)
    value_used = jnp.where(masked_flags[:, None], mask_value[None, :], values)
    query_used = jnp.where(masked_flags[:, None], rotated(mask_query, positions), queries)

    k_own = to_heads(key_used)
    v_own = to_heads(value_used)
    k_left = along_x(k_own, 1)
    k_right = along_x(k_own, -1)
    v_left = along_x(v_own, 1)
    v_right = along_x(v_own, -1)
    k_far = along_x(k_left, 1)
    v_far = along_x(v_right, -1)

    q_own = to_heads(query_used)
    q_other = other_core(q_own)
    own, own_norm = split_queries(q_own)
    other, other_norm = split_queries(q_other)

    own_state = attend(own_norm, own, [k_own], [v_own], None, "own_0")
    other_state = attend(other_norm, other, [k_own], [v_own], None, "other_0")
    near_k, near_v = [k_left, k_right], [v_left, v_right]
    own_state = attend(own_norm, own, near_k, near_v, own_state, "own_1")
    other_state = attend(other_norm, other, near_k, near_v, other_state, "other_1")
    other_state = attend(other_norm, other, [k_far], [v_far], other_state, "other_2")
    received = [other_core(x) for x in other_state[1:]]
    own_state = attend(own_norm, own, [k_far], [v_far], own_state, "own_2")
    rows = finish(own_state[1:], received)
    return lax.all_to_all(rows, PLANE, split_axis=0, concat_axis=1, tiled=True)


def solution(mesh):
    split = P(("pb", "kv", "ha"), None)
    return jax.shard_map(
        body,
        mesh=mesh,
        in_specs=(split, split, split, P(), P(), P(), P()),
        out_specs=split,
        check_vma=False,
    )
```

time: 595 us -> 503 us (0.85)
  Pallas kernels: 0 us -> 427 us
  local copies, waits for them, and re-layouts: 199 us -> 6.27 us
  waiting for transfers between devices: 131 us -> 13.1 us
  matrix products: 93.2 us -> 0 us
  other arithmetic: 67 us -> 3.03 us
  blocking collectives: 63.8 us -> 26.7 us
  between operations: 13.6 us -> 0.22 us
  starting transfers between devices: 15.9 us -> 23.8 us
    pallas_call x0 -> x9, Pallas kernels: none -> 427 us  [the longest x6 421 us: attend(): pl.pallas_call(functools.partial(attend_kernel, pieces=pieces, first=firs...]
    dynamic_update_slice x24 -> x0, local copies, waits for them, and re-layouts: 175 us -> none  [attend_piece(): lax.map(per_head, (jnp.arange(head_total, dtype=jnp.int32), head_queries,...]
    dot_general x16 -> x0, matrix products: 93.2 us -> none  [the longest x8 49.1 us: per_head(): jnp.einsum('qd,kd->qk', query_part, key_part, preferred_element_type=jnp....]
    all_to_all x3 -> x2, waiting for transfers between devices: 96.2 us -> 13 us  [to_heads(): return lax.all_to_all(x, PLANE, split_axis=1, concat_axis=0, tiled=True)]
    reduce_sum x10 -> x0, other arithmetic: 44.9 us -> none  [the longest x8 39.9 us: per_head(): new_total = old_total * factor + jnp.sum(weights, axis=1)]
    all_to_all x4 -> x2, blocking collectives: 63.8 us -> 26.7 us  [the longest x1 14.2 us: body(): return lax.all_to_all(rows, PLANE, split_axis=0, concat_axis=1, tiled=True)]
    all_gather x2 -> x0, waiting for transfers between devices: 35.1 us -> none  [the longest x1 35.1 us: side_by_side(): lax.all_gather(both, axis, axis=dim, tiled=True)]
    unnamed x2 -> x1, other arithmetic: 14.2 us -> 0.24 us
  transfers between devices with their start and end apart: 5 -> 12, of which waited for: 3 -> 2; matrix products, arithmetic and copies ran while one was open for 3% -> 0% of each run, Pallas kernels for 0% -> 74%
where the time goes in v1:
time: 503 us; the launch traced here: 500 us
  Pallas kernels  427 us (85%)
  blocking collectives  26.7 us (5%)
  starting transfers between devices  23.8 us (5%)
  waiting for transfers between devices  13.1 us (3%)
  local copies, waits for them, and re-layouts  6.27 us (1%)
    pallas_call x6, Pallas kernels, attend(): pl.pallas_call(functools.partial(attend_kernel, pieces=pieces, first=firs...  421 us
    all_to_all x1, blocking collectives, body(): return lax.all_to_all(rows, PLANE, split_axis=0, concat_axis=1, tiled=True)  14.2 us
    all_to_all x2, starting transfers between devices, to_heads(): return lax.all_to_all(x, PLANE, split_axis=1, concat_axis=0, tiled=True)  13.7 us
    all_to_all x2, waiting for transfers between devices, to_heads(): return lax.all_to_all(x, PLANE, split_axis=1, concat_axis=0, tiled=True)  13 us
    all_to_all x1, blocking collectives, to_heads(): return lax.all_to_all(x, PLANE, split_axis=1, concat_axis=0, tiled=True)  12.6 us
  transfers between devices with their start and end apart: 12, of which 2 were waited for; matrix products, arithmetic and copies ran while one was open for 0% of the time, Pallas kernels for 74%

profile of v1, /device:TPU:24, one launch (start us, length us, event | category | flops | bytes accessed | tf_op | source)
XLA Modules:
  0.0 500.3 jit_solution(11658570288602960662)
XLA Ops:
  0.0 0.7 bitcast_convert_fusion
  0.7 0.7 bitcast_convert_fusion.1
  1.4 0.2 multiply_cosine_fusion
  1.7 0.1 fusion.3
  1.7 0.4 subtract_convert_fusion
  2.2 0.0 copy-start.8
  2.2 0.2 pad_maximum_fusion
  2.4 0.0 copy-start.5
  2.4 0.0 copy-start.6
  2.4 0.0 copy-start.7
  2.4 0.0 copy-start.9
  2.4 0.2 pad_maximum_fusion.1
  2.7 0.2 copy-done.8
  2.9 0.3 compare_reduce_fusion
  3.2 0.2 copy-done.5
  3.4 0.1 copy-done.6
  3.5 0.1 copy-done.7
  3.6 0.2 select_bitcast_fusion
  3.9 0.8 copy.41
  4.7 8.2 %all-to-all-start.1 = ((bf16[96,16,128]{2,0,1:T(8,128)(2,1)}), bf16[96,16,128]{2,0,1:T(8,128)(2,1)S(1)}, u32[]{:S(2)}, u32[]{:S(2)}) async-start(bf16[96,16,128]{2,0,1:T(8,128)(2,1)} %bitcast.45), calls=%async_computation.1 | async-start | bytes 786432 | tf_op jit(solution)/shard_map/all_to_all | solution.py:235
  12.9 0.8 copy.40
  13.7 7.2 %all-to-all-done.1 = bf16[96,16,128]{2,0,1:T(8,128)(2,1)S(1)} async-done(((bf16[96,16,128]{2,0,1:T(8,128)(2,1)}), bf16[96,16,128]{2,0,1:T(8,128)(2,1)S(1)}, u32[]{:S(2)}, u32[]{:S(2)}) %all-to-all-start.1) | async-done | bytes 393248 | tf_op jit(solution)/shard_map/all_to_all | solution.py:235
  20.9 5.6 %all-to-all-start.2 = ((bf16[96,16,128]{2,0,1:T(8,128)(2,1)}), bf16[96,16,128]{2,0,1:T(8,128)(2,1)S(1)}, u32[]{:S(2)}, u32[]{:S(2)}) async-start(bf16[96,16,128]{2,0,1:T(8,128)(2,1)} %bitcast.44), calls=%async_computation.2 | async-start | bytes 786432 | tf_op jit(solution)/shard_map/all_to_all | solution.py:235
  26.5 1.5 collective-permute-start
  28.0 5.8 %all-to-all-done.2 = bf16[96,16,128]{2,0,1:T(8,128)(2,1)S(1)} async-done(((bf16[96,16,128]{2,0,1:T(8,128)(2,1)}), bf16[96,16,128]{2,0,1:T(8,128)(2,1)S(1)}, u32[]{:S(2)}, u32[]{:S(2)}) %all-to-all-start.2) | async-done | bytes 393248 | tf_op jit(solution)/shard_map/all_to_all | solution.py:235
  33.8 2.8 collective-permute-start.2
  36.5 0.1 copy.42
  36.6 12.6 %all_to_all.76 = bf16[96,16,128]{2,0,1:T(8,128)(2,1)S(1)} all-to-all(bf16[96,16,128]{2,0,1:T(8,128)(2,1)S(1)} %bitcast.58), channel_id=1, replica_groups=mesh['pb'=8,'kv'=8,'ha'=2] {'kv','ha'}, dimensions={1} | all-to-all | bytes 786432 | tf_op jit(solution)/shard_map/all_to_all | solution.py:235
  49.2 0.8 collective-permute-start.4
  50.0 1.2 collective-permute-start.5
  51.2 0.0 collective-permute-start.1
  51.2 3.2 collective-permute-start.3
  54.5 0.8 copy-done.4
  55.2 2.1 split_queries.3
  57.4 1.1 copy-done
  58.5 52.5 %other_0.1 = (s32[1,1]{1,0:T(1,128)}, f32[128,1536]{1,0:T(8,128)S(1)}, f32[8,1536]{1,0:T(8,128)}, f32[8,1536]{1,0:T(8,128)}) custom-call(f32[1,1]{1,0:T(1,128)} %get-tuple-element.44.refs_0_, bf16[1536,256]{1,0:T(8,128)(2,1)S(1)} %copy-done, bf16[1536,128]{1,0:T(8,128)(2,1)S(1)} %bitcast.49, bf16[1536,128]{1,0:T(8,128)(2,1)S(1)} %bitcast.53), custom_call_target="tpu_custom_call" | custom-call | tf_op jit(solution)/shard_map/other_0/pallas_call | solution.py:189
  111.0 104.7 %other_1.1 = (s32[1,1]{1,0:T(1,128)}, f32[128,1536]{1,0:T(8,128)S(1)}, f32[8,1536]{1,0:T(8,128)}, f32[8,1536]{1,0:T(8,128)}) custom-call(f32[1,1]{1,0:T(1,128)} %get-tuple-element.44.refs_0_, bf16[1536,256]{1,0:T(8,128)(2,1)S(1)} %copy-done.1, ...), custom_call_target="tpu_custom_call", output_to_operand_aliasing={{1}: (7, {}), {2}: (8, {}), {3}: (9, {})} | custom-call | tf_op jit(solution)/shard_map/other_1/pallas_call | solution.py:189
  215.7 54.1 %other_2.1 = (s32[1,1]{1,0:T(1,128)}, f32[128,1536]{1,0:T(8,128)S(1)}, f32[8,1536]{1,0:T(8,128)}, f32[8,1536]{1,0:T(8,128)}) custom-call(f32[1,1]{1,0:T(1,128)} %get-tuple-element.44.refs_0_, bf16[1536,256]{1,0:T(8,128)(2,1)S(1)} %copy-done.1, ...), custom_call_target="tpu_custom_call", output_to_operand_aliasing={{1}: (5, {}), {2}: (6, {}), {3}: (7, {})} | custom-call | tf_op jit(solution)/shard_map/other_2/pallas_call | solution.py:189
  269.8 0.5 collective-permute-start.8
  270.3 0.1 collective-permute-start.9
  270.4 2.1 split_queries.2
  272.5 1.1 copy-done.2
  273.7 52.3 %own_0.1 = (s32[1,1]{1,0:T(1,128)}, f32[128,1536]{1,0:T(8,128)S(1)}, f32[8,1536]{1,0:T(8,128)S(1)}, f32[8,1536]{1,0:T(8,128)S(1)}) custom-call(f32[1,1]{1,0:T(1,128)} %get-tuple-element.31.refs_0_, bf16[1536,256]{1,0:T(8,128)(2,1)S(1)} %copy-done.2, bf16[1536,128]{1,0:T(8,128)(2,1)S(1)} %bitcast.50, bf16[1536,128]{1,0:T(8,128)(2,1)S(1)} %bitcast.54), custom_call_target="tpu_custom_call" | custom-call | tf_op jit(solution)/shard_map/own_0/pallas_call | solution.py:189
  326.0 103.9 %own_1.1 = (s32[1,1]{1,0:T(1,128)}, f32[128,1536]{1,0:T(8,128)S(1)}, f32[8,1536]{1,0:T(8,128)S(1)}, f32[8,1536]{1,0:T(8,128)S(1)}) custom-call(f32[1,1]{1,0:T(1,128)} %get-tuple-element.31.refs_0_, bf16[1536,256]{1,0:T(8,128)(2,1)S(1)} %copy-done.2, ...), custom_call_target="tpu_custom_call", output_to_operand_aliasing={{1}: (7, {}), {2}: (8, {}), {3}: (9, {})} | custom-call | tf_op jit(solution)/shard_map/own_1/pallas_call | solution.py:189
  429.9 54.0 %own_2.1 = (s32[1,1]{1,0:T(1,128)}, f32[128,1536]{1,0:T(8,128)S(1)}, f32[8,1536]{1,0:T(8,128)S(1)}, f32[8,1536]{1,0:T(8,128)S(1)}) custom-call(f32[1,1]{1,0:T(1,128)} %get-tuple-element.31.refs_0_, bf16[1536,256]{1,0:T(8,128)(2,1)S(1)} %copy-done.2, ...), custom_call_target="tpu_custom_call", output_to_operand_aliasing={{1}: (5, {}), {2}: (6, {}), {3}: (7, {})} | custom-call | tf_op jit(solution)/shard_map/own_2/pallas_call | solution.py:189
  483.9 1.4 finish.1
  485.4 14.2 %all_to_all.77 = bf16[16,96,128]{2,1,0:T(8,128)(2,1)S(1)} all-to-all(bf16[16,96,128]{2,1,0:T(8,128)(2,1)S(1)} %bitcast.55), channel_id=1, replica_groups=mesh['pb'=8,'kv'=8,'ha'=2] {'kv','ha'}, dimensions={0} | all-to-all | bytes 786432 | tf_op jit(solution)/shard_map/all_to_all | solution.py:270
  499.5 0.8 copy_bitcast_fusion
  (22 shorter events, 0.1 us)
Async XLA Ops:
  2.2 0.7 copy-start.8
  2.4 1.0 copy-start.5
  2.4 1.1 copy-start.6
  2.4 1.2 copy-start.7
  2.4 1.2 copy-start.9
  4.7 16.2 %all-to-all-start.1 = ((bf16[96,16,128]{2,0,1:T(8,128)(2,1)}), bf16[96,16,128]{2,0,1:T(8,128)(2,1)S(1)}, u32[]{:S(2)}, u32[]{:S(2)}) async-start(bf16[96,16,128]{2,0,1:T(8,128)(2,1)} %bitcast.45), calls=%async_computation.1 | async-start | bytes 786432 | tf_op jit(solution)/shard_map/all_to_all | solution.py:235
  20.9 12.9 %all-to-all-start.2 = ((bf16[96,16,128]{2,0,1:T(8,128)(2,1)}), bf16[96,16,128]{2,0,1:T(8,128)(2,1)S(1)}, u32[]{:S(2)}, u32[]{:S(2)}) async-start(bf16[96,16,128]{2,0,1:T(8,128)(2,1)} %bitcast.44), calls=%async_computation.2 | async-start | bytes 786432 | tf_op jit(solution)/shard_map/all_to_all | solution.py:235
  26.5 24.7 %collective-permute-start = (bf16[1536,128]{1,0:T(8,128)(2,1)S(1)}, bf16[1536,128]{1,0:T(8,128)(2,1)S(1)}, u32[]{:S(2)}, u32[]{:S(2)}) collective-permute-start(bf16[1536,128]{1,0:T(8,128)(2,1)S(1)} %bitcast.47), channel_id=1, source_target_pairs={{0,32},{16,48},{32,64},{48,80},{64,96},{80,112},{96,0},{112,16},{1... | collective-permute-start | bytes 1179656 | tf_op jit(solution)/shard_map/ppermute | solution.py:38
  33.8 17.5 %collective-permute-start.2 = (bf16[1536,128]{1,0:T(8,128)(2,1)S(1)}, bf16[1536,128]{1,0:T(8,128)(2,1)S(1)}, u32[]{:S(2)}, u32[]{:S(2)}) collective-permute-start(bf16[1536,128]{1,0:T(8,128)(2,1)S(1)} %bitcast.51), channel_id=1, source_target_pairs={{0,96},{16,112},{32,0},{48,16},{64,32},{80,48},{96,64},{112,80},{1... | collective-permute-start | bytes 1179656 | tf_op jit(solution)/shard_map/ppermute | solution.py:38
  49.2 8.2 %copy-start.3 = (bf16[96,16,128]{2,0,1:T(8,128)(2,1)}, bf16[96,16,128]{2,0,1:T(8,128)(2,1)S(1)}, u32[]{:S(2)}) copy-start(bf16[96,16,128]{2,0,1:T(8,128)(2,1)S(1)} %all_to_all.76) | copy-start | bytes 1179652
  49.2 5.3 %collective-permute-start.6 = (bf16[1536,128]{1,0:T(8,128)(2,1)S(1)}, bf16[1536,128]{1,0:T(8,128)(2,1)S(1)}, u32[]{:S(2)}, u32[]{:S(2)}) collective-permute-start(bf16[1536,128]{1,0:T(8,128)(2,1)S(1)} %bitcast.56), channel_id=1, source_target_pairs={{0,16},{16,0},{32,48},{48,32},{64,80},{80,64},{96,112},{112,96},{1... | collective-permute-start | bytes 1179656 | tf_op jit(solution)/shard_map/ppermute | solution.py:42
  49.2 61.8 %collective-permute-start.4 = (bf16[1536,128]{1,0:T(8,128)(2,1)S(1)}, bf16[1536,128]{1,0:T(8,128)(2,1)S(1)}, u32[]{:S(2)}, u32[]{:S(2)}) collective-permute-start(bf16[1536,128]{1,0:T(8,128)(2,1)S(1)} %bitcast.48), channel_id=1, source_target_pairs={{0,96},{16,112},{32,0},{48,16},{64,32},{80,48},{96,64},{112,80},{1... | collective-permute-start | bytes 1179656 | tf_op jit(solution)/shard_map/ppermute | solution.py:38
  50.0 61.0 %collective-permute-start.5 = (bf16[1536,128]{1,0:T(8,128)(2,1)S(1)}, bf16[1536,128]{1,0:T(8,128)(2,1)S(1)}, u32[]{:S(2)}, u32[]{:S(2)}) collective-permute-start(bf16[1536,128]{1,0:T(8,128)(2,1)S(1)} %bitcast.52), channel_id=1, source_target_pairs={{0,32},{16,48},{32,64},{48,80},{64,96},{80,112},{96,0},{112,16},{1... | collective-permute-start | bytes 1179656 | tf_op jit(solution)/shard_map/ppermute | solution.py:38
  51.2 164.5 %collective-permute-start.1 = (bf16[1536,128]{1,0:T(8,128)(2,1)S(1)}, bf16[1536,128]{1,0:T(8,128)(2,1)S(1)}, u32[]{:S(2)}, u32[]{:S(2)}) collective-permute-start(bf16[1536,128]{1,0:T(8,128)(2,1)S(1)} %collective-permute-done.refs_2_), channel_id=1, source_target_pairs={{0,32},{16,48},{32,64},{48,80},{64,96},{80,112},{96,0},{112,16},{1... | collective-permute-start | bytes 1179656 | tf_op jit(solution)/shard_map/ppermute | solution.py:38
  51.2 164.5 %collective-permute-start.3 = (bf16[1536,128]{1,0:T(8,128)(2,1)S(1)}, bf16[1536,128]{1,0:T(8,128)(2,1)}, u32[]{:S(2)}, u32[]{:S(2)}) collective-permute-start(bf16[1536,128]{1,0:T(8,128)(2,1)S(1)} %collective-permute-done.2.refs_5_), channel_id=1, source_target_pairs={{0,96},{16,112},{32,0},{48,16},{64,32},{80,48},{96,64},{112,80},{1... | collective-permute-start | bytes 1179656 | tf_op jit(solution)/shard_map/ppermute | solution.py:38
  54.5 0.8 copy-start.4
  57.4 1.1 copy-start
  58.5 52.5 %copy-start.1 = (bf16[1536,256]{1,0:T(8,128)(2,1)S(1)}, bf16[1536,256]{1,0:T(8,128)(2,1)}, u32[]{:S(2)}) copy-start(bf16[1536,256]{1,0:T(8,128)(2,1)} %get-tuple-element.45.refs_1_) | copy-start | bytes 2359300
  269.8 214.1 %collective-permute-start.7 = (f32[128,1536]{1,0:T(8,128)S(1)}, f32[128,1536]{1,0:T(8,128)}, u32[]{:S(2)}, u32[]{:S(2)}) collective-permute-start(f32[128,1536]{1,0:T(8,128)S(1)} %get-tuple-element.54), channel_id=1, source_target_pairs={{0,16},{16,0},{32,48},{48,32},{64,80},{80,64},{96,112},{112,96},{1... | collective-permute-start | bytes 2359304 | tf_op jit(solution)/shard_map/ppermute | solution.py:42
  269.8 214.1 %collective-permute-start.8 = (f32[8,1536]{1,0:T(8,128)}, f32[8,1536]{1,0:T(8,128)}, u32[]{:S(2)}, u32[]{:S(2)}) collective-permute-start(f32[8,1536]{1,0:T(8,128)} %get-tuple-element.55), channel_id=1, source_target_pairs={{0,16},{16,0},{32,48},{48,32},{64,80},{80,64},{96,112},{112,96},{1... | collective-permute-start | bytes 147464 | tf_op jit(solution)/shard_map/ppermute | solution.py:42
  270.3 213.6 %collective-permute-start.9 = (f32[8,1536]{1,0:T(8,128)}, f32[8,1536]{1,0:T(8,128)}, u32[]{:S(2)}, u32[]{:S(2)}) collective-permute-start(f32[8,1536]{1,0:T(8,128)} %get-tuple-element.56), channel_id=1, source_target_pairs={{0,16},{16,0},{32,48},{48,32},{64,80},{80,64},{96,112},{112,96},{1... | collective-permute-start | bytes 147464 | tf_op jit(solution)/shard_map/ppermute | solution.py:42
  272.5 1.1 copy-start.2
